TPU v7x, 32 devices: a whole 2x2x4 slice. The times are simulated.
32 devices in a mesh: unit: 4 (over y, core), zero: 4 (over z), cols: 2 (over x).
Axes of the slice: x: 2, y: 2, z: 4, core: 2. Of those that a mesh axis runs over, the one named last changes fastest.
Arguments:
- weight_gate: bfloat16 [20480, 13824], P(('unit', 'zero'), 'cols'), parts along dimension 0, may hold values from -0.125 to 0.125
- low_gate: bfloat16 [20480, 32], P(('unit', 'zero')), parts along dimension 0, may hold values from -0.078125 to 0.078125
- high_gate: bfloat16 [128, 13824], P('unit', 'cols'), parts along dimension 0, may hold values from -1 to 1
- weight_up: bfloat16 [20480, 13824], P(('unit', 'zero'), 'cols'), parts along dimension 0, may hold values from -0.125 to 0.125
- low_up: bfloat16 [20480, 32], P(('unit', 'zero')), parts along dimension 0, may hold values from -0.078125 to 0.078125
- high_up: bfloat16 [128, 13824], P('unit', 'cols'), parts along dimension 0, may hold values from -1 to 1
- norm_train: float32 [20480], P(('unit', 'zero', 'cols')), parts along dimension 0, may hold values from 0.25 to 1.75
- norm_step: float32 [20480], P(('unit', 'zero', 'cols')), parts along dimension 0, may hold values from -0.3 to 0.3
Outputs:
- final_gate: bfloat16 [20480, 13824], P('unit', ('cols', 'zero')), parts along dimension 0
- final_up: bfloat16 [20480, 13824], P('unit', ('cols', 'zero')), parts along dimension 0
- scale_gate: float32 [55296], P(('unit', 'cols', 'zero')), parts along dimension 0
- scale_up: float32 [55296], P(('unit', 'cols', 'zero')), parts along dimension 0
- serve_norm: bfloat16 [20480], P('unit'), parts along dimension 0
There are 4 independent parts, one for each index of `unit`. A program takes and returns all parts, laid end to end along the dimension named above; each array names one. Nothing has to cross between parts.
All inputs are finite; a program needn't handle non-finite values. Where the computation divides by a largest or mean magnitude, that divisor is 1e-20 or more.
Results may differ from a plain program's by a relative error of at most 0.001.
Values may be sent and summed in bfloat16 or wider, within the bound.
A program may use at most 192 MiB of HBM per device.

v0:
```python
import jax
import jax.numpy as jnp
from jax import lax
from jax.sharding import PartitionSpec as P

D_MODEL = 5120
mix_rate = 0.5


def local(weight_gate, low_gate, high_gate, weight_up, low_up, high_up, norm_train, norm_step):
    result_gate = weight_gate.astype(jnp.float32) + mix_rate * jnp.dot(
        low_gate, high_gate, preferred_element_type=jnp.float32
    )
    result_up = weight_up.astype(jnp.float32) + mix_rate * jnp.dot(
        low_up, high_up, preferred_element_type=jnp.float32
    )
    total_gate, total_up = lax.psum(
        (jnp.sum(jnp.abs(result_gate), axis=0), jnp.sum(jnp.abs(result_up), axis=0)), "zero"
    )
    scale_gate = total_gate / D_MODEL
    scale_up = total_up / D_MODEL
    narrow_gate, narrow_up = (
        (result_gate / scale_gate).astype(jnp.bfloat16),
        (result_up / scale_up).astype(jnp.bfloat16),
    )
    final_gate, final_up = (
        lax.all_to_all(narrow_gate, "zero", split_axis=1, concat_axis=0, tiled=True),
        lax.all_to_all(narrow_up, "zero", split_axis=1, concat_axis=0, tiled=True),
    )
    place = lax.axis_index("zero")
    scale_gate = lax.dynamic_slice_in_dim(
        scale_gate, place * final_gate.shape[1], final_gate.shape[1]
    )
    scale_up = lax.dynamic_slice_in_dim(scale_up, place * final_up.shape[1], final_up.shape[1])
    serve_norm = lax.all_gather(
        (norm_train + norm_step).astype(jnp.bfloat16), ("zero", "cols"), axis=0, tiled=True
    )
    return (final_gate, final_up, scale_gate, scale_up, serve_norm)


def solution(mesh):
    in_specs = (
        P(("unit", "zero"), "cols"),
        P(("unit", "zero"), None),
        P("unit", "cols"),
        P(("unit", "zero"), "cols"),
        P(("unit", "zero"), None),
        P("unit", "cols"),
        P(("unit", "zero", "cols")),
        P(("unit", "zero", "cols")),
    )
    out_specs = (
        P("unit", ("cols", "zero")),
        P("unit", ("cols", "zero")),
        P(("unit", "cols", "zero")),
        P(("unit", "cols", "zero")),
        P("unit"),
    )
    return jax.shard_map(local, mesh=mesh, in_specs=in_specs, out_specs=out_specs, check_vma=False)
```

profile of v0, /device:TPU:0, one launch (start us, length us, event | category | flops | bytes accessed | tf_op | source)
XLA Modules:
  0.0 996.0 jit_solution(447909113472326274)
XLA Ops:
  0.6 0.0 copy-start
  0.6 0.0 copy-start.3
  0.7 0.0 copy-start.2
  0.7 1.0 copy-done
  1.7 17.9 %abs_reduce_fusion.1 = (f32[6912]{0:T(1024)S(1)}, f32[1280,6912]{1,0:T(8,128)}) fusion(bf16[1280,32]{0,1:T(8,128)(2,1)} %param.9, bf16[32,6912]{1,0:T(8,128)(2,1)S(1)} %copy-done, bf16[1280,6912]{1,0:T(8,128)(2,1)} %param.8), kind=kOutput, calls=%fused_computation.4 | convolution fusion | flops 610460928 | bytes 53636096 | tf_op jit(solution)/shard_map/dot_general | solution.py:11
  19.6 18.0 %abs_reduce_fusion = (f32[6912]{0:T(1024)S(1)}, f32[1280,6912]{1,0:T(8,128)}) fusion(bf16[1280,32]{0,1:T(8,128)(2,1)S(1)} %copy-done.3, bf16[32,6912]{1,0:T(8,128)(2,1)S(1)} %copy-done.2, bf16[1280,6912]{1,0:T(8,128)(2,1)} %param.11), kind=kOutput, calls=%fused_computation.1 | convolution fusion | flops 610460928 | bytes 53636096 | tf_op jit(solution)/shard_map/dot_general | solution.py:14
  37.6 21.7 %all-reduce = (f32[6912]{0:T(1024)S(1)}, f32[6912]{0:T(1024)S(1)}) all-reduce(f32[6912]{0:T(1024)S(1)} %get-tuple-element.17, f32[6912]{0:T(1024)S(1)} %get-tuple-element.19), channel_id=1, replica_groups=mesh['unit'=4,'zero'=4,'cols'=2] {'zero'}, use_global_device_ids=true, to_apply=%region_1.0 | all-reduce | flops 13824 | bytes 110592 | tf_op jit(solution)/shard_map/psum | solution.py:17
  59.3 19.8 %divide_convert_fusion.1 = bf16[1280,6912]{1,0:T(8,128)(2,1)} fusion(f32[1280,6912]{1,0:T(8,128)} %get-tuple-element.18, f32[6912]{0:T(1024)S(1)} %get-tuple-element.22), kind=kLoop, calls=%fused_computation.3 | loop fusion | flops 17694720 | bytes 53111808 | tf_op jit(solution)/shard_map/convert_element_type | solution.py:23
  79.1 24.6 %copy.23 = bf16[1280,6912]{0,1:T(8,128)(2,1)} copy(bf16[1280,6912]{1,0:T(8,128)(2,1)} %divide_convert_fusion.1) | data formatting | bytes 35389440 | tf_op jit(solution)/shard_map/convert_element_type | solution.py:23
  103.7 7.2 all-to-all-start
  110.9 19.8 %divide_convert_fusion = bf16[1280,6912]{1,0:T(8,128)(2,1)} fusion(f32[1280,6912]{1,0:T(8,128)} %get-tuple-element.20, f32[6912]{0:T(1024)S(1)} %get-tuple-element.21), kind=kLoop, calls=%fused_computation | loop fusion | flops 17694720 | bytes 53111808 | tf_op jit(solution)/shard_map/convert_element_type | solution.py:24
  130.7 23.0 %copy.25 = bf16[1280,6912]{0,1:T(8,128)(2,1)} copy(bf16[1280,6912]{1,0:T(8,128)(2,1)} %divide_convert_fusion) | data formatting | bytes 35389440 | tf_op jit(solution)/shard_map/convert_element_type | solution.py:24
  153.7 335.9 %all-to-all-done = bf16[1280,4,1728]{0,2,1:T(8,128)(2,1)} async-done(((bf16[1280,4,1728]{0,2,1:T(8,128)(2,1)}), bf16[1280,4,1728]{0,2,1:T(8,128)(2,1)}, u32[]{:S(2)}, u32[]{:S(2)}) %all-to-all-start) | async-done | bytes 17694752 | tf_op jit(solution)/shard_map/all_to_all | solution.py:27
  489.6 7.2 all-to-all-start.1
  496.8 0.7 dynamic_slice.6
  497.5 0.7 dynamic_slice.7
  498.2 400.5 %all-gather = bf16[8,1,640]{2,1,0:T(2,128)(2,1)S(1)} all-gather(bf16[1,1,640]{2,1,0:T(2,128)(2,1)S(1)} %reshape.18), channel_id=1, replica_groups=mesh['unit'=4,'zero'=4,'cols'=2] {'zero','cols'}, dimensions={0}, use_global_device_ids=true | all-gather | bytes 11520 | tf_op jit(solution)/shard_map/all_gather | solution.py:35
  898.8 0.1 reduce
  898.8 0.6 reshape.19
  899.4 23.3 %copy.24 = bf16[4,1280,1728]{2,1,0:T(8,128)(2,1)} copy(bf16[4,1280,1728]{1,2,0:T(8,128)(2,1)} %bitcast.1) | data formatting | bytes 35389440 | tf_op jit(solution)/shard_map/all_to_all | solution.py:27
  922.8 24.9 %copy.27 = bf16[5120,1728]{0,1:T(8,128)(2,1)} copy(bf16[5120,1728]{1,0:T(8,128)(2,1)} %bitcast.10) | data formatting | bytes 35389440
  947.7 0.0 all-to-all-done.1
  947.7 23.4 %copy.26 = bf16[4,1280,1728]{2,1,0:T(8,128)(2,1)} copy(bf16[4,1280,1728]{1,2,0:T(8,128)(2,1)} %bitcast.4) | data formatting | bytes 35389440 | tf_op jit(solution)/shard_map/all_to_all | solution.py:28
  971.1 24.9 %copy.28 = bf16[5120,1728]{0,1:T(8,128)(2,1)} copy(bf16[5120,1728]{1,0:T(8,128)(2,1)} %bitcast.11) | data formatting | bytes 35389440
  (11 shorter events, 0.0 us)
Async XLA Ops:
  0.6 1.0 copy-start
  0.6 18.9 %copy-start.3 = (bf16[1280,32]{0,1:T(8,128)(2,1)S(1)}, bf16[1280,32]{0,1:T(8,128)(2,1)}, u32[]{:S(2)}) copy-start(bf16[1280,32]{0,1:T(8,128)(2,1)} %param.12) | copy-start | bytes 245764
  0.7 18.9 %copy-start.2 = (bf16[32,6912]{1,0:T(8,128)(2,1)S(1)}, bf16[32,6912]{1,0:T(8,128)(2,1)}, u32[]{:S(2)}) copy-start(bf16[32,6912]{1,0:T(8,128)(2,1)} %param.13) | copy-start | bytes 1327108
  103.7 385.9 %all-to-all-start = ((bf16[1280,4,1728]{0,2,1:T(8,128)(2,1)}), bf16[1280,4,1728]{0,2,1:T(8,128)(2,1)}, u32[]{:S(2)}, u32[]{:S(2)}) async-start(bf16[1280,4,1728]{0,2,1:T(8,128)(2,1)} %bitcast.13), calls=%async_computation | async-start | bytes 35389440 | tf_op jit(solution)/shard_map/all_to_all | solution.py:27
  130.7 367.5 %copy-start.4 = (f32[640]{0:T(1024)S(1)}, f32[640]{0:T(1024)}, u32[]{:S(2)}) copy-start(f32[640]{0:T(1024)} %param.14) | copy-start | bytes 7684
  130.7 367.5 %copy-start.5 = (f32[640]{0:T(1024)S(1)}, f32[640]{0:T(1024)}, u32[]{:S(2)}) copy-start(f32[640]{0:T(1024)} %param.15) | copy-start | bytes 7684
  489.6 458.1 %all-to-all-start.1 = ((bf16[1280,4,1728]{0,2,1:T(8,128)(2,1)}), bf16[1280,4,1728]{0,2,1:T(8,128)(2,1)}, u32[]{:S(2)}, u32[]{:S(2)}) async-start(bf16[1280,4,1728]{0,2,1:T(8,128)(2,1)} %bitcast.12), calls=%async_computation.1 | async-start | bytes 35389440 | tf_op jit(solution)/shard_map/all_to_all | solution.py:28
  947.7 48.3 %copy-start.1 = (bf16[32,6912]{1,0:T(8,128)(2,1)S(1)}, bf16[32,6912]{1,0:T(8,128)(2,1)}, u32[]{:S(2)}) copy-start(bf16[32,6912]{1,0:T(8,128)(2,1)} %param.10) | copy-start | bytes 1327108
where the time goes:
time: 1000 us; the launch traced here: 996 us
  blocking collectives  422 us (42%)
  waiting for transfers between devices  336 us (34%)
  local copies, waits for them, and re-layouts  147 us (15%)
  other arithmetic  39.7 us (4%)
  matrix products  35.9 us (4%)
  starting transfers between devices  14.4 us (1%)
    all_gather x1, blocking collectives, local(): lax.all_gather((norm_train + norm_step).astype(jnp.bfloat16), ('zero', 'c...  401 us
    all_to_all x1, waiting for transfers between devices, local(): lax.all_to_all(narrow_gate, 'zero', split_axis=1, concat_axis=0, tiled=True)  336 us
    unnamed x16, local copies, waits for them, and re-layouts  51.5 us
    convert_element_type x1, local copies, waits for them, and re-layouts, local(): (result_gate / scale_gate).astype(jnp.bfloat16)  24.6 us
    all_to_all x1, local copies, waits for them, and re-layouts, local(): lax.all_to_all(narrow_up, 'zero', split_axis=1, concat_axis=0, tiled=True)  23.4 us
    all_to_all x1, local copies, waits for them, and re-layouts, local(): lax.all_to_all(narrow_gate, 'zero', split_axis=1, concat_axis=0, tiled=True)  23.3 us
    convert_element_type x1, local copies, waits for them, and re-layouts, local(): (result_up / scale_up).astype(jnp.bfloat16)  23 us
    psum x1, blocking collectives, local(): lax.psum((jnp.sum(jnp.abs(result_gate), axis=0), jnp.sum(jnp.abs(result_u...  21.7 us
  transfers between devices with their start and end apart: 2, of which 1 were waited for; matrix products, arithmetic and copies ran while one was open for 9% of the time, Pallas kernels for 0%

commit v1 on v0

--- a/solution.py
+++ b/solution.py
@@ -2,6 +2,7 @@
 import jax.numpy as jnp
 from jax import lax
 from jax.sharding import PartitionSpec as P
+from jax.lax import all_to_all, psum
 
 D_MODEL = 5120
 mix_rate = 0.5
@@ -32,8 +33,16 @@
         scale_gate, place * final_gate.shape[1], final_gate.shape[1]
     )
     scale_up = lax.dynamic_slice_in_dim(scale_up, place * final_up.shape[1], final_up.shape[1])
-    serve_norm = lax.all_gather(
-        (norm_train + norm_step).astype(jnp.bfloat16), ("zero", "cols"), axis=0, tiled=True
+    serve_norm = jnp.concatenate(
+        all_to_all(
+            jnp.stack(
+                [(norm_train + norm_step).astype(jnp.bfloat16)] * psum(1, ("zero", "cols")), 0
+            ),
+            ("zero", "cols"),
+            0,
+            0,
+        ),
+        0,
     )
     return (final_gate, final_up, scale_gate, scale_up, serve_norm)
 

time: 1000 us -> 938 us (0.938)
  blocking collectives: 422 us -> 20.1 us
  waiting for transfers between devices: 336 us -> 667 us
    all_gather x1 -> x0, blocking collectives: 401 us -> none  [local(): lax.all_gather((norm_train + norm_step).astype(jnp.bfloat16), ('zero', 'c...]
    all_to_all x1, waiting for transfers between devices: 0.01 us -> 332 us  [local(): lax.all_to_all(narrow_up, 'zero', split_axis=1, concat_axis=0, tiled=True)]
    unnamed x16 -> x12, local copies, waits for them, and re-layouts: 51.5 us -> 50.6 us
  transfers between devices with their start and end apart: 2 -> 3, of which waited for: 1 -> 2; matrix products, arithmetic and copies ran while one was open for 9% -> 19% of each run, Pallas kernels for 0% -> 0%
where the time goes in v1:
time: 938 us; the launch traced here: 934 us
  waiting for transfers between devices  667 us (71%)
  local copies, waits for them, and re-layouts  147 us (16%)
  other arithmetic  41.1 us (4%)
  matrix products  35.8 us (4%)
  starting transfers between devices  21.6 us (2%)
  blocking collectives  20.1 us (2%)
    all_to_all x1, waiting for transfers between devices, local(): lax.all_to_all(narrow_gate, 'zero', split_axis=1, concat_axis=0, tiled=True)  336 us
    all_to_all x1, waiting for transfers between devices, local(): lax.all_to_all(narrow_up, 'zero', split_axis=1, concat_axis=0, tiled=True)  332 us
    unnamed x12, local copies, waits for them, and re-layouts  50.6 us
    convert_element_type x1, local copies, waits for them, and re-layouts, local(): (result_gate / scale_gate).astype(jnp.bfloat16)  24.6 us
    all_to_all x1, local copies, waits for them, and re-layouts, local(): lax.all_to_all(narrow_up, 'zero', split_axis=1, concat_axis=0, tiled=True)  23.4 us
    all_to_all x1, local copies, waits for them, and re-layouts, local(): lax.all_to_all(narrow_gate, 'zero', split_axis=1, concat_axis=0, tiled=True)  23.3 us
    convert_element_type x1, local copies, waits for them, and re-layouts, local(): (result_up / scale_up).astype(jnp.bfloat16)  23 us
    psum x1, blocking collectives, local(): lax.psum((jnp.sum(jnp.abs(result_gate), axis=0), jnp.sum(jnp.abs(result_u...  20.1 us
  transfers between devices with their start and end apart: 3, of which 2 were waited for; matrix products, arithmetic and copies ran while one was open for 19% of the time, Pallas kernels for 0%

profile of v1, /device:TPU:0, one launch (start us, length us, event | category | flops | bytes accessed | tf_op | source)
XLA Modules:
  0.0 934.2 jit_solution(2332191974616088017)
XLA Ops:
  0.7 0.8 add_convert_fusion
  1.5 0.5 broadcast.21
  2.0 0.7 reduce.1
  2.7 0.7 reshape.31
  3.4 7.3 all-to-all-start.2
  10.7 17.9 %abs_reduce_fusion.1 = (f32[6912]{0:T(1024)S(1)}, f32[1280,6912]{1,0:T(8,128)}) fusion(bf16[1280,32]{0,1:T(8,128)(2,1)} %param.9, bf16[32,6912]{1,0:T(8,128)(2,1)S(1)} %copy-done, bf16[1280,6912]{1,0:T(8,128)(2,1)} %param.8), kind=kOutput, calls=%fused_computation.4 | convolution fusion | flops 610460928 | bytes 53636096 | tf_op jit(solution)/shard_map/dot_general | solution.py:12
  28.6 17.9 %abs_reduce_fusion = (f32[6912]{0:T(1024)S(1)}, f32[1280,6912]{1,0:T(8,128)}) fusion(bf16[1280,32]{0,1:T(8,128)(2,1)S(1)} %copy-done.3, bf16[32,6912]{1,0:T(8,128)(2,1)S(1)} %copy-done.2, bf16[1280,6912]{1,0:T(8,128)(2,1)} %param.11), kind=kOutput, calls=%fused_computation.1 | convolution fusion | flops 610460928 | bytes 53636096 | tf_op jit(solution)/shard_map/dot_general | solution.py:15
  46.5 20.1 %all-reduce = (f32[6912]{0:T(1024)S(1)}, f32[6912]{0:T(1024)S(1)}) all-reduce(f32[6912]{0:T(1024)S(1)} %get-tuple-element.17, f32[6912]{0:T(1024)S(1)} %get-tuple-element.19), channel_id=1, replica_groups=mesh['unit'=4,'zero'=4,'cols'=2] {'zero'}, use_global_device_ids=true, to_apply=%region_1.0 | all-reduce | flops 13824 | bytes 110592 | tf_op jit(solution)/shard_map/psum | solution.py:18
  66.7 19.8 %divide_convert_fusion.1 = bf16[1280,6912]{1,0:T(8,128)(2,1)} fusion(f32[1280,6912]{1,0:T(8,128)} %get-tuple-element.18, f32[6912]{0:T(1024)S(1)} %get-tuple-element.22), kind=kLoop, calls=%fused_computation.3 | loop fusion | flops 17694720 | bytes 53111808 | tf_op jit(solution)/shard_map/convert_element_type | solution.py:24
  86.4 24.6 %copy.23 = bf16[1280,6912]{0,1:T(8,128)(2,1)} copy(bf16[1280,6912]{1,0:T(8,128)(2,1)} %divide_convert_fusion.1) | data formatting | bytes 35389440 | tf_op jit(solution)/shard_map/convert_element_type | solution.py:24
  111.1 7.2 all-to-all-start
  118.2 19.8 %divide_convert_fusion = bf16[1280,6912]{1,0:T(8,128)(2,1)} fusion(f32[1280,6912]{1,0:T(8,128)} %get-tuple-element.20, f32[6912]{0:T(1024)S(1)} %get-tuple-element.21), kind=kLoop, calls=%fused_computation | loop fusion | flops 17694720 | bytes 53111808 | tf_op jit(solution)/shard_map/convert_element_type | solution.py:25
  138.0 23.0 %copy.25 = bf16[1280,6912]{0,1:T(8,128)(2,1)} copy(bf16[1280,6912]{1,0:T(8,128)(2,1)} %divide_convert_fusion) | data formatting | bytes 35389440 | tf_op jit(solution)/shard_map/convert_element_type | solution.py:25
  161.0 335.7 %all-to-all-done = bf16[1280,4,1728]{0,2,1:T(8,128)(2,1)} async-done(((bf16[1280,4,1728]{0,2,1:T(8,128)(2,1)}), bf16[1280,4,1728]{0,2,1:T(8,128)(2,1)}, u32[]{:S(2)}, u32[]{:S(2)}) %all-to-all-start) | async-done | bytes 17694752 | tf_op jit(solution)/shard_map/all_to_all | solution.py:28
  496.7 7.2 all-to-all-start.1
  503.9 0.7 dynamic_slice.6
  504.6 0.7 dynamic_slice.7
  505.3 0.1 reshape.32
  505.4 0.6 reshape.29
  506.0 23.3 %copy.24 = bf16[4,1280,1728]{2,1,0:T(8,128)(2,1)} copy(bf16[4,1280,1728]{1,2,0:T(8,128)(2,1)} %bitcast.1) | data formatting | bytes 35389440 | tf_op jit(solution)/shard_map/all_to_all | solution.py:28
  529.3 24.9 %copy.27 = bf16[5120,1728]{0,1:T(8,128)(2,1)} copy(bf16[5120,1728]{1,0:T(8,128)(2,1)} %bitcast.10) | data formatting | bytes 35389440
  554.3 331.7 %all-to-all-done.1 = bf16[1280,4,1728]{0,2,1:T(8,128)(2,1)} async-done(((bf16[1280,4,1728]{0,2,1:T(8,128)(2,1)}), bf16[1280,4,1728]{0,2,1:T(8,128)(2,1)}, u32[]{:S(2)}, u32[]{:S(2)}) %all-to-all-start.1) | async-done | bytes 17694752 | tf_op jit(solution)/shard_map/all_to_all | solution.py:29
  886.0 23.4 %copy.26 = bf16[4,1280,1728]{2,1,0:T(8,128)(2,1)} copy(bf16[4,1280,1728]{1,2,0:T(8,128)(2,1)} %bitcast.4) | data formatting | bytes 35389440 | tf_op jit(solution)/shard_map/all_to_all | solution.py:29
  909.3 24.9 %copy.28 = bf16[5120,1728]{0,1:T(8,128)(2,1)} copy(bf16[5120,1728]{1,0:T(8,128)(2,1)} %bitcast.11) | data formatting | bytes 35389440
  (12 shorter events, 0.1 us)
Async XLA Ops:
  0.6 10.0 %copy-start = (bf16[32,6912]{1,0:T(8,128)(2,1)S(1)}, bf16[32,6912]{1,0:T(8,128)(2,1)}, u32[]{:S(2)}) copy-start(bf16[32,6912]{1,0:T(8,128)(2,1)} %param.10) | copy-start | bytes 1327108
  0.6 28.0 %copy-start.3 = (bf16[1280,32]{0,1:T(8,128)(2,1)S(1)}, bf16[1280,32]{0,1:T(8,128)(2,1)}, u32[]{:S(2)}) copy-start(bf16[1280,32]{0,1:T(8,128)(2,1)} %param.12) | copy-start | bytes 245764
  0.7 28.0 %copy-start.2 = (bf16[32,6912]{1,0:T(8,128)(2,1)S(1)}, bf16[32,6912]{1,0:T(8,128)(2,1)}, u32[]{:S(2)}) copy-start(bf16[32,6912]{1,0:T(8,128)(2,1)} %param.13) | copy-start | bytes 1327108
  3.4 107.7 %all-to-all-start.2 = ((bf16[8,2,320]{2,1,0:T(2,128)(2,1)}), bf16[8,2,320]{2,1,0:T(2,128)(2,1)S(1)}, u32[]{:S(2)}, u32[]{:S(2)}) async-start(bf16[8,2,320]{2,1,0:T(2,128)(2,1)} %reshape.31), calls=%async_computation.2 | async-start | bytes 24576 | tf_op jit(solution)/shard_map/all_to_all | solution.py:37
  111.1 385.6 %all-to-all-start = ((bf16[1280,4,1728]{0,2,1:T(8,128)(2,1)}), bf16[1280,4,1728]{0,2,1:T(8,128)(2,1)}, u32[]{:S(2)}, u32[]{:S(2)}) async-start(bf16[1280,4,1728]{0,2,1:T(8,128)(2,1)} %bitcast.13), calls=%async_computation | async-start | bytes 35389440 | tf_op jit(solution)/shard_map/all_to_all | solution.py:28
  496.7 389.3 %all-to-all-start.1 = ((bf16[1280,4,1728]{0,2,1:T(8,128)(2,1)}), bf16[1280,4,1728]{0,2,1:T(8,128)(2,1)}, u32[]{:S(2)}, u32[]{:S(2)}) async-start(bf16[1280,4,1728]{0,2,1:T(8,128)(2,1)} %bitcast.12), calls=%async_computation.1 | async-start | bytes 35389440 | tf_op jit(solution)/shard_map/all_to_all | solution.py:29
  886.0 48.3 %copy-start.1 = (bf16[32,6912]{1,0:T(8,128)(2,1)S(1)}, bf16[32,6912]{1,0:T(8,128)(2,1)}, u32[]{:S(2)}) copy-start(bf16[32,6912]{1,0:T(8,128)(2,1)} %param.10) | copy-start | bytes 1327108
